TPU v7x, 32 devices: a whole 2x2x4 slice. The times are simulated.
32 devices in a mesh: rep: 8 (over y, x, core), tp: 4 (over z).
Axes of the slice: x: 2, y: 2, z: 4, core: 2. Of those that a mesh axis runs over, the one named last changes fastest.
Arguments:
- tokens: bfloat16 [8192, 1280], P(('rep', 'tp')), may hold values from -6 to 6
- view_ids: int32 [32, 4], P('rep'), may hold values from 0 to 31
- time_ids: int32 [32], P('rep'), may hold values from 0 to 999
- camera_table: float32 [32, 1280], replicated, may hold values from -6 to 6
- norm_attn: float32 [2, 1280], replicated, may hold values from 0.1 to 1.9
- norm_ffn: float32 [2, 1280], replicated, may hold values from 0.1 to 1.9
- w_query: bfloat16 [2, 1280, 1280], P(None, ('rep', 'tp')), may hold values from -0.1677051 to 0.1677051
- w_key: bfloat16 [2, 1280, 1280], P(None, ('rep', 'tp')), may hold values from -6.764106 to 6.764106
- w_value: bfloat16 [2, 1280, 1280], P(None, ('rep', 'tp')), may hold values from -0.15625 to 0.15625
- w_out: bfloat16 [2, 1280, 1280], P(None, ('rep', 'tp')), may hold values from -0.15625 to 0.15625
- w_gate: bfloat16 [2, 1280, 5120], P(None, ('rep', 'tp')), may hold values from -0.15625 to 0.15625
- w_up: bfloat16 [2, 1280, 5120], P(None, ('rep', 'tp')), may hold values from -0.15625 to 0.15625
- w_down: bfloat16 [2, 1280, 5120], P(None, ('rep', 'tp')), may hold values from -0.078125 to 0.078125
Outputs:
- denoised: bfloat16 [8192, 1280], P(('rep', 'tp'))
All inputs are finite; a program needn't handle non-finite values.
Results may differ from a plain program's by a relative error of at most 0.035.
Values may be sent and summed in bfloat16 or wider, within the bound.
A program may use at most 128 MiB of HBM per device.

v0:
```python
import functools
import math

import jax
import jax.numpy as jnp
from jax import lax
from jax.experimental import pallas as pl
from jax.experimental.pallas import tpu as pltpu
from jax.sharding import PartitionSpec as P

D = 1280
HEADS = 8
VIEWS = 4
HW = 64
LAYERS = 2


def layer_norm(activations, gain_vector):
    average = jnp.mean(activations, axis=-1, keepdims=True)
    centred = activations - average
    spread = jnp.mean(centred * centred, axis=-1, keepdims=True)
    return (centred * lax.rsqrt(spread + 1e-05) * gain_vector).astype(jnp.bfloat16)


def time_code(step_ids, width):
    half_width = width // 2
    frequency = jnp.exp(-math.log(10000.0) * jnp.arange(half_width, dtype=jnp.float32) / half_width)
    angles = step_ids.astype(jnp.float32)[:, None] * frequency[None, :]
    return jnp.concatenate([jnp.cos(angles), jnp.sin(angles)], axis=1)


def conditioning(row_ids, view_ids, time_ids, camera_table):
    set_ids = row_ids // (VIEWS * HW)
    slot_ids = set_ids * VIEWS + row_ids // HW % VIEWS
    flat_views = view_ids.reshape(-1)
    slot_range = jnp.arange(flat_views.shape[0], dtype=jnp.int32)
    pose_ids = jnp.sum(
        jnp.where(slot_ids[:, None] == slot_range[None, :], flat_views[None, :], 0), axis=1
    )
    set_range = jnp.arange(time_ids.shape[0], dtype=jnp.int32)
    step_ids = jnp.sum(
        jnp.where(set_ids[:, None] == set_range[None, :], time_ids[None, :], 0), axis=1
    )
    pose_range = jnp.arange(camera_table.shape[0], dtype=jnp.int32)
    onehot_pose = (pose_ids[:, None] == pose_range[None, :]).astype(jnp.float32)
    camera = jnp.dot(onehot_pose, camera_table, precision=lax.Precision.HIGHEST)
    return camera + time_code(step_ids, camera_table.shape[1])


CLASSES = (("xyz", 9), ("yxz", 9), ("zxy", 31), ("zyx", 31))


def class_columns(width):
    total = sum(share for _, share in CLASSES)
    lanes = width // 128
    bounds, spent = [0], 0
    for _, share in CLASSES:
        spent += share
        bounds.append(lanes * spent // total * 128)
    return [(bounds[i], bounds[i + 1] - bounds[i]) for i in range(len(CLASSES))]


def routes(lengths):
    found = []
    for kind, (order, _) in enumerate(CLASSES):
        spans = {axis: range(1 - lengths[axis], lengths[axis]) for axis in "yz"}
        spans["x"] = range(0, 2)
        for dx in spans["x"]:
            for dy in spans["y"]:
                for dz in spans["z"]:
                    hops = abs(dx) + abs(dy) + abs(dz)
                    found.append((hops, kind, {"x": dx, "y": dy, "z": dz}))
    found.sort(key=lambda item: item[0])
    return found


def send_plan(lengths):
    plan = []
    for hops, kind, offset in routes(lengths):
        order = CLASSES[kind][0]
        last = max([i for i in range(3) if offset[order[i]] != 0], default=-1)
        targets = []
        if last >= 0 and order[last] != "x":
            targets.append((order[last], 1 if offset[order[last]] < 0 else -1))
        for axis in order[last + 1 :]:
            targets += [("x", 1)] if axis == "x" else [(axis, 1), (axis, -1)]
        targets.append(("core", 1))
        plan.append((hops, kind, offset, targets))
    return plan


def gather_kernel(lengths, layers, shard_count, *refs):
    shard_refs, full_refs = refs[:shard_count], refs[shard_count : shard_count + layers]
    packed_ref, pack_sem, own_sem, send_sems, recv_sems = refs[shard_count + layers :]
    packing, column = [], 0
    for index, shard_ref in enumerate(shard_refs):
        size = shard_ref.shape[2]
        packing.append(
            pltpu.make_async_copy(
                shard_ref, packed_ref.at[:, :, pl.ds(column, size)], pack_sem.at[index]
            )
        )
        packing[-1].start()
        column += size
    tp_count = lengths["z"]
    rep_here = lax.axis_index("rep")
    here = {
        "z": lax.axis_index("tp"),
        "y": rep_here // 4,
        "x": rep_here // 2 % 2,
        "core": rep_here % 2,
    }
    columns = class_columns(packed_ref.shape[2])

    def device(place):
        return (place["y"] * 4 + place["x"] * 2 + place["core"], place["z"])

    def moved(place, axis, step):
        place = dict(place)
        place[axis] = 1 - place[axis] if axis in ("x", "core") else place[axis] + step
        return place

    def exists(axis, step):
        if axis in ("x", "core"):
            return None
        return here[axis] < lengths[axis] - 1 if step > 0 else here[axis] > 0

    def both(first, second):
        if first is None or second is None:
            return second if first is None else first
        return jnp.logical_and(first, second)

    def guarded(condition, action):
        if condition is None:
            action()
        else:
            pl.when(condition)(action)

    barrier = pltpu.get_barrier_semaphore()
    neighbours = [("core", 1), ("x", 1), ("y", 1), ("y", -1), ("z", 1), ("z", -1)]
    for axis, step in neighbours:
        def greet(axis=axis, step=step):
            pl.semaphore_signal(
                barrier, inc=1, device_id=device(moved(here, axis, step)),
                device_id_type=pl.DeviceIdType.MESH,
            )
        guarded(exists(axis, step), greet)
    count = jnp.int32(2)
    for axis in "yz":
        count = count + (here[axis] > 0).astype(jnp.int32)
        count = count + (here[axis] < lengths[axis] - 1).astype(jnp.int32)
    pl.semaphore_wait(barrier, count)

    for copy in packing:
        copy.wait()
    my_rep, my_tp = device(here)
    own_copies = [
        pltpu.make_async_copy(
            packed_ref.at[layer], full_refs[layer].at[my_rep * tp_count + my_tp], own_sem.at[layer]
        )
        for layer in range(layers)
    ]
    for copy in own_copies:
        copy.start()

    finish = []
    plan = send_plan(lengths)

    def run(layer, item):
        hops, kind, offset, targets = item
        start, size = columns[kind]
        source = dict(here)
        valid = None
        for axis in "yz":
            source[axis] = here[axis] + offset[axis]
            if offset[axis] > 0:
                valid = both(valid, source[axis] < lengths[axis])
            elif offset[axis] < 0:
                valid = both(valid, source[axis] >= 0)
        if offset["x"]:
            source["x"] = 1 - here["x"]
        rep_from, tp_from = device(source)
        block = rep_from * tp_count + tp_from
        span = pl.ds(start, size)
        landed = full_refs[layer].at[block, :, span]
        origin = packed_ref.at[layer, :, span] if hops == 0 else landed
        arrived = recv_sems.at[layer * len(CLASSES) + kind, block]
        sends = []
        for axis, step in targets:
            copy = pltpu.make_async_remote_copy(
                src_ref=origin,
                dst_ref=landed,
                send_sem=send_sems.at[len(finish) + len(sends)],
                recv_sem=arrived,
                device_id=device(moved(here, axis, step)),
                device_id_type=pl.DeviceIdType.MESH,
            )
            sends.append((both(valid, exists(axis, step)), copy, exists(axis, step)))

        def action():
            if hops:
                sends[-1][1].wait_recv()
            for _, copy, there in sends:
                guarded(there, copy.start)

        guarded(valid, action)
        finish.extend((condition, copy.wait_send) for condition, copy, _ in sends)

        def from_sibling():
            other = dict(source)
            other["core"] = 1 - here["core"]
            rep_other, tp_other = device(other)
            block_other = rep_other * tp_count + tp_other
            there = full_refs[layer].at[block_other, :, span]
            pltpu.make_async_remote_copy(
                src_ref=there,
                dst_ref=there,
                send_sem=send_sems.at[0],
                recv_sem=recv_sems.at[layer * len(CLASSES) + kind, block_other],
                device_id=device(moved(here, "core", 1)),
                device_id_type=pl.DeviceIdType.MESH,
            ).wait_recv()

        finish.append((valid, from_sibling))

    own = [item for item in plan if item[0] == 0]
    rest = [item for item in plan if item[0] > 0]
    for item in own:
        run(0, item)
    for layer in range(layers):
        early = len(rest) // 5
        for item in rest[:early]:
            run(layer, item)
        if layer + 1 < layers:
            for item in own:
                run(layer + 1, item)
        for item in rest[early:]:
            run(layer, item)
    for condition, action in finish:
        guarded(condition, action)
    for copy in own_copies:
        copy.wait()


def gather_weights(shards, rep_count, tp_count):
    layers, rows, _ = shards[0].shape
    width = sum(shard.shape[2] for shard in shards)
    kind = shards[0].dtype
    devices = rep_count * tp_count
    lengths = {"x": 2, "y": rep_count // 4, "z": tp_count}
    slots = layers * sum(len(item[3]) + 1 for item in send_plan(lengths))
    full = pl.pallas_call(
        functools.partial(gather_kernel, lengths, layers, len(shards)),
        out_shape=[jax.ShapeDtypeStruct((devices, rows, width), kind)] * layers,
        in_specs=[pl.BlockSpec(memory_space=pl.ANY)] * len(shards),
        out_specs=[pl.BlockSpec(memory_space=pl.ANY)] * layers,
        scratch_shapes=[
            pltpu.VMEM((layers, rows, width), kind),
            pltpu.SemaphoreType.DMA((len(shards),)),
            pltpu.SemaphoreType.DMA((layers,)),
            pltpu.SemaphoreType.DMA((slots,)),
            pltpu.SemaphoreType.DMA((layers * len(CLASSES), devices)),
        ],
        compiler_params=pltpu.CompilerParams(collective_id=0, has_side_effects=True),
        name="gather_weights",
    )(*shards)
    return [one.reshape(devices * rows, width) for one in full]


def attend(packed, head_size):
    total_rows = packed.shape[0]
    width = packed.shape[1] // 3
    set_rows = VIEWS * HW
    query_rows, sources = packed[:, :width], packed[:, width:]
    if total_rows % set_rows != 0:
        first = lax.axis_index("tp") * total_rows // set_rows * set_rows
        sources = lax.all_gather(sources, "tp", axis=0, tiled=True)
        sources = lax.dynamic_slice_in_dim(sources, first, set_rows, 0)
    set_count = sources.shape[0] // set_rows
    query_rows = query_rows.reshape(set_count, -1, width // head_size, head_size)
    key_rows = sources[:, :width].reshape(set_count, set_rows, -1, head_size)
    value_rows = sources[:, width:].reshape(set_count, set_rows, -1, head_size)
    scores = jnp.einsum(
        "bqhd,bkhd->bhqk", query_rows, key_rows, preferred_element_type=jnp.float32
    ) * head_size ** (-0.5)
    peak = jnp.max(scores, axis=-1, keepdims=True)
    expons = jnp.exp(scores - peak)
    attn_probs = (expons / jnp.sum(expons, axis=-1, keepdims=True)).astype(jnp.bfloat16)
    mixed_rows = jnp.einsum(
        "bhqk,bkhd->bqhd", attn_probs, value_rows, preferred_element_type=jnp.float32
    )
    return mixed_rows.astype(jnp.bfloat16).reshape(total_rows, width)


def out_terms(mixed_rows, weight):
    return lax.dot_general(
        mixed_rows, weight, (((1,), (1,)), ((), ())), preferred_element_type=jnp.float32
    )


def ffn_kernel(steps, stream_ref, gain_ref, gate_ref, up_ref, down_ref, out_ref, normed, total):
    step = pl.program_id(0)

    @pl.when(step == 0)
    def _():
        normed[...] = layer_norm(stream_ref[...], gain_ref[...])
        total[...] = stream_ref[...]

    gate_part = jnp.dot(normed[...], gate_ref[...], preferred_element_type=jnp.float32)
    up_part = jnp.dot(normed[...], up_ref[...], preferred_element_type=jnp.float32)
    gate_part = 0.5 * gate_part * (1.0 + lax.erf(gate_part * math.sqrt(0.5)))
    hidden = (gate_part * up_part).astype(jnp.bfloat16)
    total[...] += out_terms(hidden, down_ref[...])

    @pl.when(step == steps - 1)
    def _():
        out_ref[...] = total[...].astype(out_ref.dtype)


def feed_forward(stream, gain_vector, weights, first, inner, out_dtype):
    rows, width = stream.shape
    tile = 512 if inner % 512 == 0 and first % 512 == 0 else 128
    steps = inner // tile
    depth = weights.shape[0]

    def columns(which):
        base = (first + which * inner) // tile
        return pl.BlockSpec((depth, tile), lambda step: (0, base + step))

    return pl.pallas_call(
        functools.partial(ffn_kernel, steps),
        grid=(steps,),
        out_shape=jax.ShapeDtypeStruct((rows, width), out_dtype),
        in_specs=[
            pl.BlockSpec((rows, width), lambda step: (0, 0)),
            pl.BlockSpec((1, width), lambda step: (0, 0)),
            columns(0),
            columns(1),
            columns(2),
        ],
        out_specs=pl.BlockSpec((rows, width), lambda step: (0, 0)),
        scratch_shapes=[
            pltpu.VMEM((rows, width), jnp.bfloat16),
            pltpu.VMEM((rows, width), jnp.float32),
        ],
        compiler_params=pltpu.CompilerParams(dimension_semantics=("arbitrary",)),
        cost_estimate=pl.CostEstimate(
            flops=6 * rows * width * inner,
            bytes_accessed=6 * depth * inner,
            transcendentals=rows * inner,
        ),
        name="feed_forward",
    )(stream, gain_vector[None], weights, weights, weights)


def body(
    tokens,
    view_ids,
    time_ids,
    camera_table,
    norm_attn,
    norm_ffn,
    w_query,
    w_key,
    w_value,
    w_out,
    w_gate,
    w_up,
    w_down,
):
    tp_count = lax.axis_size("tp")
    rep_count = lax.axis_size("rep")
    width = w_query.shape[2]
    inner = w_gate.shape[2]
    head_size = D // HEADS
    shards = (w_query, w_key, w_value, w_out, w_gate, w_up, w_down)
    one_kernel = rep_count % 4 == 0 and rep_count * tp_count * LAYERS * len(CLASSES) <= 256
    if one_kernel:
        weights = gather_weights(shards, rep_count, tp_count)
    share_rows = tokens.shape[0]
    row_ids = lax.axis_index("tp") * share_rows + jnp.arange(share_rows, dtype=jnp.int32)
    stream = tokens.astype(jnp.float32) + conditioning(row_ids, view_ids, time_ids, camera_table)

    def whole_weight(layer_index, first, count, after):
        if one_kernel:
            start = sum(shard.shape[2] for shard in shards[:first])
            size = sum(shard.shape[2] for shard in shards[first : first + count])
            return weights[layer_index][:, start : start + size]
        own = [shard[layer_index] for shard in shards[first : first + count]]
        own, _ = lax.optimization_barrier((own, after))
        return lax.all_gather(jnp.concatenate(own, axis=1), ("rep", "tp"), axis=0, tiled=True)

    for layer_index in range(LAYERS):
        normed = layer_norm(stream, norm_attn[layer_index])
        qkv_w = whole_weight(layer_index, 0, 3, normed)
        packed = jnp.dot(normed, qkv_w, preferred_element_type=jnp.float32).astype(jnp.bfloat16)
        mixed_rows = attend(packed, head_size)
        stream = stream + out_terms(mixed_rows, whole_weight(layer_index, 3, 1, mixed_rows))
        if one_kernel:
            stream = feed_forward(
                stream,
                norm_ffn[layer_index],
                weights[layer_index],
                4 * width,
                inner,
                jnp.bfloat16 if layer_index == LAYERS - 1 else jnp.float32,
            )
            continue
        normed = layer_norm(stream, norm_ffn[layer_index])
        gate_w = whole_weight(layer_index, 4, 1, normed)
        gate_part = jnp.dot(normed, gate_w, preferred_element_type=jnp.float32)
        up_w = whole_weight(layer_index, 5, 1, gate_part)
        up_part = jnp.dot(normed, up_w, preferred_element_type=jnp.float32)
        hidden = (jax.nn.gelu(gate_part, approximate=False) * up_part).astype(jnp.bfloat16)
        stream = stream + out_terms(hidden, whole_weight(layer_index, 6, 1, hidden))
    return stream.astype(jnp.bfloat16)


def solution(mesh):
    return jax.shard_map(
        body,
        mesh=mesh,
        in_specs=(
            P(("rep", "tp"), None),
            P("rep", None),
            P("rep"),
            P(),
            P(),
            P(),
            P(None, ("rep", "tp"), None),
            P(None, ("rep", "tp"), None),
            P(None, ("rep", "tp"), None),
            P(None, ("rep", "tp"), None),
            P(None, ("rep", "tp"), None),
            P(None, ("rep", "tp"), None),
            P(None, ("rep", "tp"), None),
        ),
        out_specs=P(("rep", "tp"), None),
        check_vma=False,
    )
```

profile of v0, /device:TPU:0, one launch (start us, length us, event | category | flops | bytes accessed | tf_op | source)
XLA Modules:
  0.0 469.3 jit_solution(6148465108458620177)
XLA Ops:
  0.0 0.0 copy-start
  0.0 0.8 select_reduce_fusion.1
  0.8 2.3 multiply_cosine_fusion
  3.2 0.8 broadcast_in_dim.26
  3.9 0.1 select_reduce_fusion
  4.0 0.0 copy-done
  4.0 2.0 fusion.46
  6.0 0.0 copy-start.5
  6.1 384.2 %gather_weights.1 = (bf16[32,40,20480]{2,1,0:T(8,128)(2,1)}, bf16[32,40,20480]{2,1,0:T(8,128)(2,1)}) custom-call(bf16[2,40,1280]{2,1,0:T(8,128)(2,1)} %refs_0_.1, bf16[2,40,1280]{2,1,0:T(8,128)(2,1)} %refs_1_.1, bf16[2,40,1280]{2,1,0:T(8,128)(2,1)} %refs_2_.1, bf16[2,40,1280]{2,1,0:T(8,128)(2,1)} %refs_3_.1, bf16[2,40,5120]{2,1,0:T(8,128)(2,1)} %refs_4_.1, ...), custom_call_target="tpu_custom_call" | custom-call | tf_op jit(solution)/shard_map/gather_weights/pallas_call | solution.py:252
  390.3 0.0 copy-done.5
  390.4 0.3 multiply_reduce_fusion.3
  390.7 6.6 %fusion.6 = bf16[256,3840]{1,0:T(8,128)(2,1)S(1)} fusion(bf16[1280,20480]{1,0:T(8,128)(2,1)} %bitcast.32, f32[256,1280]{1,0:T(8,128)S(1)} %get-tuple-element.22, f32[1280]{0:T(1024)S(1)} %get-tuple-element.10, f32[256]{0:T(256)S(1)} %add_rsqrt_fusion.1, f32[256]{0:T(256)S(1)} %broadcast_multiply_fusion.1), kind=kOutput, calls=%fused_computation.6 | convolution fusion | flops 2518876160 | bytes 13114368 | tf_op jit(solution)/shard_map/dot_general | solution.py:396
  397.3 0.1 fusion.44
  397.4 1.1 copy.30
  398.5 0.2 copy.31
  398.7 0.2 copy.32
  399.0 0.0 copy-start.3
  399.0 2.2 fusion.47
  401.1 0.0 copy-done.3
  401.1 1.9 convolution_convert_fusion.1
  403.1 0.0 copy-start.6
  403.1 4.1 fusion.17.stream_ref
  407.2 0.0 copy-done.6
  407.2 0.6 fusion.45
  407.8 21.5 %feed_forward.2 = f32[256,1280]{1,0:T(8,128)} custom-call(f32[256,1280]{1,0:T(8,128)} %fusion.17.stream_ref, f32[1,1280]{1,0:T(1,128)} %get-tuple-element.18.gain_ref, bf16[1280,20480]{1,0:T(8,128)(2,1)} %bitcast.34, bf16[1280,20480]{1,0:T(8,128)(2,1)} %bitcast.35, bf16[1280,20480]{1,0:T(8,128)(2,1)} %bitcast.36), custom_call_target="tpu_custom_call" | custom-call | flops 10066329600 | bytes 39321600 | tf_op jit(solution)/shard_map/feed_forward/pallas_call | solution.py:330
  429.4 0.0 copy-start.2
  429.4 1.6 reduce_sum.77
  430.9 0.1 copy-done.2
  431.1 0.3 multiply_reduce_fusion.2
  431.4 6.6 %fusion.9 = bf16[256,3840]{1,0:T(8,128)(2,1)S(1)} fusion(bf16[1280,20480]{1,0:T(8,128)(2,1)} %bitcast.27, f32[256,1280]{1,0:T(8,128)S(1)} %copy-done.2, f32[1280]{0:T(1024)S(1)} %get-tuple-element.9, f32[256]{0:T(256)S(1)} %add_rsqrt_fusion, f32[256]{0:T(256)S(1)} %broadcast_multiply_fusion), kind=kOutput, calls=%fused_computation.7 | convolution fusion | flops 2518876160 | bytes 13114368 | tf_op jit(solution)/shard_map/dot_general | solution.py:396
  438.0 0.1 fusion.43
  438.1 1.1 copy.34
  439.2 0.2 copy.35
  439.4 0.2 copy.36
  439.7 0.0 copy-start.4
  439.7 2.2 fusion.48
  441.9 0.0 copy-done.4
  441.9 1.9 convolution_convert_fusion
  443.8 4.1 fusion.20.stream_ref
  448.0 0.0 copy-start.1
  448.0 21.3 %feed_forward.3 = bf16[256,1280]{1,0:T(8,128)(2,1)} custom-call(f32[256,1280]{1,0:T(8,128)} %fusion.20.stream_ref, f32[1,1280]{1,0:T(1,128)} %get-tuple-element.17.gain_ref, bf16[1280,20480]{1,0:T(8,128)(2,1)} %bitcast.29, bf16[1280,20480]{1,0:T(8,128)(2,1)} %bitcast.30, bf16[1280,20480]{1,0:T(8,128)(2,1)} %bitcast.31), custom_call_target="tpu_custom_call" | custom-call | flops 10066329600 | bytes 39321600 | tf_op jit(solution)/shard_map/feed_forward/pallas_call | solution.py:330
  469.3 0.0 copy-done.1
  (8 shorter events, 0.1 us)
Async XLA Ops:
  0.0 4.0 copy-start
  6.0 384.3 %copy-start.5 = (f32[2,1280]{1,0:T(2,128)S(1)}, f32[2,1280]{1,0:T(2,128)}, u32[]{:S(2)}) copy-start(f32[2,1280]{1,0:T(2,128)} %param.17) | copy-start | bytes 30724
  399.0 2.2 copy-start.3
  403.1 4.1 copy-start.6
  429.4 1.7 copy-start.2
  439.7 2.2 copy-start.4
  448.0 21.3 %copy-start.1 = (f32[32,1280]{1,0:T(8,128)S(1)}, f32[32,1280]{1,0:T(8,128)}, u32[]{:S(2)}) copy-start(f32[32,1280]{1,0:T(8,128)} %param.16) | copy-start | bytes 491524
where the time goes:
time: 470 us; the launch traced here: 469 us
  Pallas kernels  427 us (91%)
  matrix products  31.7 us (7%)
  other arithmetic  5.37 us (1%)
  local copies, waits for them, and re-layouts  4.93 us (1%)
    pallas_call x1, Pallas kernels, gather_weights(): pl.pallas_call(functools.partial(gather_kernel, lengths, layers, len(shar...  384 us
    pallas_call x2, Pallas kernels, feed_forward(): pl.pallas_call(functools.partial(ffn_kernel, steps), grid=(steps,), out_s...  42.9 us
    dot_general x2, matrix products, body(): jnp.dot(normed, qkv_w, preferred_element_type=jnp.float32)  13.2 us

commit v1 on v0

v1 whole, which is shorter than its diff:
```python
import functools
import math

import jax
import jax.numpy as jnp
from jax import lax
from jax.experimental import pallas as pl
from jax.experimental.pallas import tpu as pltpu
from jax.sharding import PartitionSpec as P

D = 1280
HEADS = 8
VIEWS = 4
HW = 64
LAYERS = 2


def layer_norm(activations, gain_vector):
    average = jnp.mean(activations, axis=-1, keepdims=True)
    centred = activations - average
    spread = jnp.mean(centred * centred, axis=-1, keepdims=True)
    return (centred * lax.rsqrt(spread + 1e-05) * gain_vector).astype(jnp.bfloat16)


def time_code(step_ids, width):
    half_width = width // 2
    frequency = jnp.exp(-math.log(10000.0) * jnp.arange(half_width, dtype=jnp.float32) / half_width)
    angles = step_ids.astype(jnp.float32)[:, None] * frequency[None, :]
    return jnp.concatenate([jnp.cos(angles), jnp.sin(angles)], axis=1)


def conditioning(row_ids, view_ids, time_ids, camera_table):
    set_ids = row_ids // (VIEWS * HW)
    slot_ids = set_ids * VIEWS + row_ids // HW % VIEWS
    flat_views = view_ids.reshape(-1)
    slot_range = jnp.arange(flat_views.shape[0], dtype=jnp.int32)
    pose_ids = jnp.sum(
        jnp.where(slot_ids[:, None] == slot_range[None, :], flat_views[None, :], 0), axis=1
    )
    set_range = jnp.arange(time_ids.shape[0], dtype=jnp.int32)
    step_ids = jnp.sum(
        jnp.where(set_ids[:, None] == set_range[None, :], time_ids[None, :], 0), axis=1
    )
    pose_range = jnp.arange(camera_table.shape[0], dtype=jnp.int32)
    onehot_pose = (pose_ids[:, None] == pose_range[None, :]).astype(jnp.float32)
    camera = jnp.dot(onehot_pose, camera_table, precision=lax.Precision.HIGHEST)
    return camera + time_code(step_ids, camera_table.shape[1])


MESH = pl.DeviceIdType.MESH
LANES = 128
PLANE = 4


class Pieces:
    def __init__(self, chips_z, layers, tile_count, send_sems):
        self.chips_z, self.layers, self.tile_count = chips_z, layers, tile_count
        self.send_sems = send_sems
        self.used = 0
        self.finish = []
        rep_here = lax.axis_index("rep")
        self.z = lax.axis_index("tp")
        self.q = rep_here // 2
        self.core = rep_here % 2
        flip_x = self.q + 1 - 2 * (self.q % 2)
        flip_y = (self.q + 2) % PLANE
        self.first = flip_x + self.core * (flip_y - flip_x)
        self.second = flip_y + self.core * (flip_x - flip_y)
        self.diagonal = PLANE - 1 - self.q

    def at(self, q, core, z):
        return (q * 2 + core, z)

    def sibling(self):
        return self.at(self.q, 1 - self.core, self.z)

    def peer(self, q):
        return self.at(q, self.core, self.z)

    def line(self, step):
        return self.at(self.q, self.core, self.z + step)

    def copy(self, source, target, arrived, device, condition=None, later=True):
        one = pltpu.make_async_remote_copy(
            src_ref=source,
            dst_ref=target,
            send_sem=self.send_sems.at[self.used],
            recv_sem=arrived,
            device_id=device,
            device_id_type=MESH,
        )
        self.used += 1
        if later:
            self.finish.append((condition, one))
        return one

    def arrival(self, region, arrived):
        pltpu.make_async_remote_copy(
            src_ref=region,
            dst_ref=region,
            send_sem=self.send_sems.at[0],
            recv_sem=arrived,
            device_id=self.sibling(),
            device_id_type=MESH,
        ).wait_recv()


def both(first, second):
    if first is None or second is None:
        return second if first is None else first
    return jnp.logical_and(first, second)


def guarded(condition, action):
    if condition is None:
        action()
    else:
        pl.when(condition)(action)


def fused_kernel(
    shape,
    tokens_ref,
    cond_ref,
    gain_attn_ref,
    gain_ffn_ref,
    wq_ref,
    wk_ref,
    wv_ref,
    wo_ref,
    wg_ref,
    wu_ref,
    wd_ref,
    out_ref,
    full,
    normed,
    landing,
    staging,
    total,
    stream,
    own_sems,
    send_sems,
    line_sems,
    plane_sems,
    share_sems,
    pair_attn_sems,
    pair_ffn_sems,
    rows_sems,
    term_sems,
):
    layers, chips_z, width, tile, tile_count, head_size = shape
    net = Pieces(chips_z, layers, tile_count, send_sems)
    z, q, core = net.z, net.q, net.core
    rows = stream.shape[0]
    here = core * chips_z + z

    def attn_piece(layer, q_from, core_from, z_from):
        return full.at[layer, 0:4, q_from, core_from * chips_z + z_from]

    def ffn_piece(layer, part, core_from, z_from):
        return full.at[
            layer, 4:7, :, core_from * chips_z + z_from, :, pl.ds(part * tile, tile)
        ]

    def in_line(offset):
        if offset == 0:
            return None
        return z + offset < chips_z if offset > 0 else z + offset >= 0

    def beyond(step):
        return z < chips_z - 1 if step > 0 else z > 0

    own = []
    for layer in range(layers):
        group = []
        for kind, ref in enumerate((wq_ref, wk_ref, wv_ref, wo_ref)):
            group.append((ref.at[layer], full.at[layer, kind, q, here]))
        own.append(group)
    for layer in range(layers):
        group = []
        for kind, ref in enumerate((wg_ref, wu_ref, wd_ref)):
            group.append(
                (ref.at[layer, :, pl.ds(q * width, width)], full.at[layer, 4 + kind, q, here])
            )
        own.append(group)
    local, slot = [], 0
    for group in own:
        copies = []
        for source, target in group:
            copies.append(pltpu.make_async_copy(source, target, own_sems.at[slot]))
            copies[-1].start()
            slot += 1
        local.append(copies)

    def wait_local(index):
        for one in local[index]:
            one.wait()

    barrier = pltpu.get_barrier_semaphore()
    for device in (
        net.sibling(),
        net.peer(net.first),
        net.peer(net.second),
        net.peer(net.diagonal),
    ):
        pl.semaphore_signal(barrier, inc=1, device_id=device, device_id_type=MESH)
    for step in (1, -1):
        def greet(step=step):
            pl.semaphore_signal(barrier, inc=1, device_id=net.line(step), device_id_type=MESH)
        pl.when(beyond(step))(greet)
    count = jnp.int32(4) + (z > 0).astype(jnp.int32) + (z < chips_z - 1).astype(jnp.int32)
    pl.semaphore_wait(barrier, count)

    def along_line(stage, region, pair_sem, offset):
        z_from = z + offset
        valid = in_line(offset)
        sends = []
        for step in (1, -1):
            if offset == 0 or (offset > 0) == (step < 0):
                ahead = beyond(step)
                one = net.copy(
                    region,
                    region,
                    line_sems.at[stage, z_from],
                    net.line(step),
                    both(valid, ahead),
                )
                sends.append((ahead, one))
        share = net.copy(region, region, pair_sem, net.sibling(), valid)

        def action():
            if offset:
                net.arrival(region, line_sems.at[stage, z_from])
            for ahead, one in sends:
                guarded(ahead, one.start)
            share.start()

        guarded(valid, action)

    def attn_line(layer, offset):
        along_line(
            layer,
            attn_piece(layer, q, core, z + offset),
            pair_attn_sems.at[layer, q, z + offset],
            offset,
        )

    def attn_plane(layer, offset):
        z_from = z + offset
        valid = in_line(offset)
        region = attn_piece(layer, q, core, z_from)
        sends = [
            net.copy(region, region, plane_sems.at[layer, q, z_from], net.peer(peer), valid)
            for peer in (net.first, net.second)
        ]

        def action():
            for one in sends:
                one.start()

        guarded(valid, action)

    def from_plane(layer, offset, which):
        z_from = z + offset
        valid = in_line(offset)
        peer = (net.first, net.second, net.diagonal)[which]
        region = attn_piece(layer, peer, core, z_from)
        arrived = plane_sems.at[layer, peer, z_from]
        sends = []
        if which == 0:
            sends.append(net.copy(region, region, arrived, net.peer(net.second), valid))
        sends.append(
            net.copy(
                region, region, pair_attn_sems.at[layer, peer, z_from], net.sibling(), valid
            )
        )

        def action():
            net.arrival(region, arrived)
            for one in sends:
                one.start()

        guarded(valid, action)

    def attn_pairs(layer):
        def wait_one(index, carry):
            q_from, z_from = index // chips_z, index % chips_z
            net.arrival(
                attn_piece(layer, q_from, 1 - core, z_from),
                pair_attn_sems.at[layer, q_from, z_from],
            )
            return carry

        lax.fori_loop(0, PLANE * chips_z, wait_one, 0)

    def exchange_columns(layer):
        for peer in (net.first, net.second, net.diagonal):
            for kind, ref in enumerate((wg_ref, wu_ref, wd_ref)):
                net.copy(
                    ref.at[layer, :, pl.ds(peer * width, width)],
                    full.at[layer, 4 + kind, q, here],
                    share_sems.at[layer, q],
                    net.peer(peer),
                ).start()

    def columns_here(layer):
        wait_local(layers + layer)
        for peer in (net.first, net.second, net.diagonal):
            net.arrival(full.at[layer, 4:7, peer, here], share_sems.at[layer, peer])

    def ffn_line(layer, part, offset):
        along_line(
            layers + layer * tile_count + part,
            ffn_piece(layer, part, core, z + offset),
            pair_ffn_sems.at[layer * tile_count + part, z + offset],
            offset,
        )

    def ffn_pairs(layer, part):
        for z_from in range(chips_z):
            net.arrival(
                ffn_piece(layer, part, 1 - core, z_from),
                pair_ffn_sems.at[layer * tile_count + part, z_from],
            )

    def offsets(hops):
        return [hops, -hops] if hops else [0]

    steps = []
    for layer in range(layers):
        steps.append(("attn", layer, 0))
    for layer in range(layers):
        for part in range(tile_count):
            steps.append(("ffn", layer, part))

    def send_own(step):
        kind, layer, part = step
        if kind == "attn":
            wait_local(layer)
            attn_line(layer, 0)
        else:
            if part == 0:
                columns_here(layer)
            ffn_line(layer, part, 0)

    def pass_on(step, hops):
        kind, layer, part = step
        for offset in offsets(hops):
            if kind == "attn":
                attn_line(layer, offset)
            else:
                ffn_line(layer, part, offset)

    queue = []
    for index, step in enumerate(steps):
        if index == 0:
            queue.append((step, 0))
        for hops in range(1, chips_z):
            if hops == 2 and index + 1 < len(steps):
                queue.append((steps[index + 1], 0))
            queue.append((step, hops))
    done = [0]

    def pump(amount):
        for _ in range(amount):
            if done[0] < len(queue):
                step, hops = queue[done[0]]
                done[0] += 1
                if hops == 0:
                    send_own(step)
                else:
                    pass_on(step, hops)

    def pump_until(step):
        while (step, chips_z - 1) in queue[done[0] :]:
            pump(1)

    plane_queue = []
    for layer in range(layers):
        items = []
        for hops in range(chips_z):
            items.append((2 * hops, "out", layer, hops))
            items.append((2 * hops + 1, "near", layer, hops))
            items.append((2 * hops + 2.5, "far", layer, hops))
        items.sort(key=lambda item: item[0])
        plane_queue.append(items)
    plane_done = [0] * layers

    def spread(layer, amount):
        for _ in range(amount):
            if plane_done[layer] == len(plane_queue[layer]):
                return
            _, what, _, hops = plane_queue[layer][plane_done[layer]]
            plane_done[layer] += 1
            for offset in offsets(hops):
                if what == "out":
                    attn_plane(layer, offset)
                elif what == "near":
                    from_plane(layer, offset, 0)
                    from_plane(layer, offset, 1)
                else:
                    from_plane(layer, offset, 2)

    chunk = 64 if rows % 64 == 0 else rows

    def normalise(gain_ref, layer):
        def one(index, carry):
            span = pl.ds(pl.multiple_of(index * chunk, chunk), chunk)
            normed[0, span, :] = layer_norm(stream[span, :], gain_ref[layer : layer + 1, :])
            return carry

        lax.fori_loop(0, rows // chunk, one, 0)

    def weight(layer, kind, index, size):
        span = pl.ds(pl.multiple_of(index * size, size), size)
        return full[layer, kind, :, :, :, span].reshape(width, size)

    column = 256 if width % 256 == 0 else LANES

    def project(layer, kind):
        def one(index, carry):
            span = pl.ds(pl.multiple_of(index * column, column), column)
            staging[kind, :, span] = jnp.dot(
                normed[0], weight(layer, kind, index, column), preferred_element_type=jnp.float32
            ).astype(jnp.bfloat16)
            return carry

        lax.fori_loop(0, width // column, one, 0)

    window = head_window(head_size)

    def attend_heads(first_head, last_head):
        def one(head, carry):
            start = head * head_size
            base = pl.multiple_of(start // LANES * LANES, LANES)
            span = pl.ds(base, window)
            lane = lax.broadcasted_iota(jnp.int32, (1, window), 1) + base
            inside = jnp.logical_and(lane >= start, lane < start + head_size)
            query = staging[0, :, span]
            scores = out_terms(
                jnp.where(inside, query, jnp.zeros_like(query)), staging[1, :, span]
            ) * head_size ** (-0.5)
            peak = jnp.max(scores, axis=-1, keepdims=True)
            expons = jnp.exp(scores - peak)
            probs = (expons / jnp.sum(expons, axis=-1, keepdims=True)).astype(jnp.bfloat16)
            mixed = jnp.dot(
                probs, staging[2, :, span], preferred_element_type=jnp.float32
            ).astype(jnp.bfloat16)
            staging[0, :, span] = jnp.where(inside, mixed, query)
            return carry

        lax.fori_loop(first_head, last_head, one, 0)

    def project_out(layer):
        def one(index, carry):
            span = pl.ds(pl.multiple_of(index * column, column), column)
            stream[...] += out_terms(staging[0, :, span], weight(layer, 3, index, column))
            return carry

        lax.fori_loop(0, width // column, one, 0)

    def ffn_tile(layer, part, place):
        gate = jnp.dot(
            normed[place], weight(layer, 4, part, tile), preferred_element_type=jnp.float32
        )
        up = jnp.dot(
            normed[place], weight(layer, 5, part, tile), preferred_element_type=jnp.float32
        )
        gate = 0.5 * gate * (1.0 + lax.erf(gate * math.sqrt(0.5)))
        hidden = (gate * up).astype(jnp.bfloat16)
        term = out_terms(hidden, weight(layer, 6, part, tile))
        if part == 0:
            total[place] = term
        else:
            total[place] = total[place] + term

    pump(1)
    spread(0, 1)
    exchange_columns(0)
    views = cond_ref.shape[0]
    per_view = rows // views
    for view in range(views):
        span = pl.ds(view * per_view, per_view)
        stream[span, :] = tokens_ref[span, :].astype(jnp.float32) + cond_ref[view : view + 1, :]
    normalise(gain_attn_ref, 0)

    pump(1)
    spread(0, 1)
    pump(2)
    spread(0, 2)
    spread(0, 1)
    pump(1)
    spread(0, 2)
    pump(1)
    spread(0, 2)
    pump(1)
    spread(0, 20)
    pump(1)
    attn_pairs(0)

    for layer in range(layers):
        last_layer = layer == layers - 1
        if layer:
            pump_until(("attn", layer, 0))
            spread(layer, 20)
            attn_pairs(layer)
            normalise(gain_attn_ref, layer)
        project(layer, 0)
        project(layer, 1)
        project(layer, 2)
        pump(1)
        if not last_layer:
            pump_until(("attn", layer + 1, 0))
            exchange_columns(layer + 1)
            spread(layer + 1, 3)
        attend_heads(0, D // head_size)
        pump(1)
        project_out(layer)
        normalise(gain_ffn_ref, layer)

        rows_sent = [
            net.copy(
                normed.at[0],
                normed.at[1 + side],
                rows_sems.at[layer, side],
                net.peer((net.first, net.second)[side]),
                later=False,
            )
            for side in range(2)
        ]
        for one in rows_sent:
            one.start()
        pump(2)
        net.arrival(normed.at[1], rows_sems.at[layer, 0])
        rows_sent.append(
            net.copy(
                normed.at[1],
                normed.at[3],
                rows_sems.at[layer, 2],
                net.peer(net.second),
                later=False,
            )
        )
        rows_sent[-1].start()
        if not last_layer:
            spread(layer + 1, 3)
        pump(1)
        net.arrival(normed.at[2], rows_sems.at[layer, 1])
        pump(1)

        for part in range(tile_count - 1):
            pump_until(("ffn", layer, part))
            ffn_pairs(layer, part)
            if part == 0:
                net.arrival(normed.at[3], rows_sems.at[layer, 2])

            def one(place, carry, part=part):
                ffn_tile(layer, part, place)
                return carry

            lax.fori_loop(0, PLANE, one, 0)
        for sent in rows_sent:
            sent.wait_send()
        part = tile_count - 1
        pump_until(("ffn", layer, part))
        ffn_pairs(layer, part)

        terms_sent = []

        def send_term(slot, target, arrived, peer):
            terms_sent.append(
                net.copy(
                    staging.at[slot], landing.at[target], arrived, net.peer(peer), later=False
                )
            )
            terms_sent[-1].start()

        ffn_tile(layer, part, 3)
        staging[0] = total[3].astype(jnp.bfloat16)
        send_term(0, 0, term_sems.at[layer, 0], net.first)
        ffn_tile(layer, part, 1)
        staging[1] = total[1].astype(jnp.bfloat16)
        send_term(1, 1, term_sems.at[layer, 1], net.first)
        ffn_tile(layer, part, 2)
        net.arrival(landing.at[0], term_sems.at[layer, 0])
        staging[2] = (total[2] + landing[0].astype(jnp.float32)).astype(jnp.bfloat16)
        send_term(2, 2, term_sems.at[layer, 2], net.second)
        ffn_tile(layer, part, 0)
        pump(2)
        net.arrival(landing.at[1], term_sems.at[layer, 1])
        pump(1)
        net.arrival(landing.at[2], term_sems.at[layer, 2])

        def add(index, carry, last_layer=last_layer):
            span = pl.ds(pl.multiple_of(index * chunk, chunk), chunk)
            summed = stream[span, :] + (
                total[0, span, :]
                + landing[1, span, :].astype(jnp.float32)
                + landing[2, span, :].astype(jnp.float32)
            )
            if last_layer:
                out_ref[span, :] = summed.astype(out_ref.dtype)
            else:
                stream[span, :] = summed
            return carry

        lax.fori_loop(0, rows // chunk, add, 0)
        for sent in terms_sent:
            sent.wait_send()

    for condition, one in net.finish:
        guarded(condition, one.wait_send)


def head_window(head_size):
    reach = head_size + LANES - math.gcd(head_size, LANES)
    return -(-reach // LANES) * LANES


def fused_blocks(tokens, cond, norm_attn, norm_ffn, shards, chips_z):
    layers, share, width = shards[0].shape
    inner = shards[4].shape[2]
    tile = 256 if width % 256 == 0 else LANES
    tile_count = width // tile
    rows = tokens.shape[0]
    head_size = D // HEADS
    stages = layers * (1 + tile_count)
    sends = 1024
    shape = (layers, chips_z, width, tile, tile_count, head_size)
    anywhere = pl.BlockSpec(memory_space=pl.ANY)
    inside = pl.BlockSpec(memory_space=pltpu.VMEM)
    kind = tokens.dtype
    return pl.pallas_call(
        functools.partial(fused_kernel, shape),
        out_shape=jax.ShapeDtypeStruct((rows, width), kind),
        in_specs=[inside] * 4 + [anywhere] * 7,
        out_specs=inside,
        scratch_shapes=[
            pltpu.VMEM((layers, 7, PLANE, 2 * chips_z, share, width), kind),
            pltpu.VMEM((PLANE, rows, width), kind),
            pltpu.VMEM((3, rows, width), kind),
            pltpu.VMEM((3, rows, width), kind),
            pltpu.VMEM((PLANE, rows, width), jnp.float32),
            pltpu.VMEM((rows, width), jnp.float32),
            pltpu.SemaphoreType.DMA((layers * 7,)),
            pltpu.SemaphoreType.DMA((sends,)),
            pltpu.SemaphoreType.DMA((stages, chips_z)),
            pltpu.SemaphoreType.DMA((layers, PLANE, chips_z)),
            pltpu.SemaphoreType.DMA((layers, PLANE)),
            pltpu.SemaphoreType.DMA((layers, PLANE, chips_z)),
            pltpu.SemaphoreType.DMA((layers * tile_count, chips_z)),
            pltpu.SemaphoreType.DMA((layers, 3)),
            pltpu.SemaphoreType.DMA((layers, 3)),
        ],
        compiler_params=pltpu.CompilerParams(
            collective_id=0, has_side_effects=True, vmem_limit_bytes=67_000_000
        ),
        name="fused_blocks",
    )(tokens, cond, norm_attn, norm_ffn, *shards)


def attend(packed, head_size):
    total_rows = packed.shape[0]
    width = packed.shape[1] // 3
    set_rows = VIEWS * HW
    query_rows, sources = packed[:, :width], packed[:, width:]
    if total_rows % set_rows != 0:
        first = lax.axis_index("tp") * total_rows // set_rows * set_rows
        sources = lax.all_gather(sources, "tp", axis=0, tiled=True)
        sources = lax.dynamic_slice_in_dim(sources, first, set_rows, 0)
    set_count = sources.shape[0] // set_rows
    query_rows = query_rows.reshape(set_count, -1, width // head_size, head_size)
    key_rows = sources[:, :width].reshape(set_count, set_rows, -1, head_size)
    value_rows = sources[:, width:].reshape(set_count, set_rows, -1, head_size)
    scores = jnp.einsum(
        "bqhd,bkhd->bhqk", query_rows, key_rows, preferred_element_type=jnp.float32
    ) * head_size ** (-0.5)
    peak = jnp.max(scores, axis=-1, keepdims=True)
    expons = jnp.exp(scores - peak)
    attn_probs = (expons / jnp.sum(expons, axis=-1, keepdims=True)).astype(jnp.bfloat16)
    mixed_rows = jnp.einsum(
        "bhqk,bkhd->bqhd", attn_probs, value_rows, preferred_element_type=jnp.float32
    )
    return mixed_rows.astype(jnp.bfloat16).reshape(total_rows, width)


def out_terms(mixed_rows, weight):
    return lax.dot_general(
        mixed_rows, weight, (((1,), (1,)), ((), ())), preferred_element_type=jnp.float32
    )


def set_conditioning(view_ids, time_ids, camera_table):
    pose_range = jnp.arange(camera_table.shape[0], dtype=jnp.int32)
    onehot_pose = (view_ids[0][:, None] == pose_range[None, :]).astype(jnp.float32)
    camera = jnp.dot(onehot_pose, camera_table, precision=lax.Precision.HIGHEST)
    return camera + time_code(time_ids, camera_table.shape[1])


def body(
    tokens,
    view_ids,
    time_ids,
    camera_table,
    norm_attn,
    norm_ffn,
    w_query,
    w_key,
    w_value,
    w_out,
    w_gate,
    w_up,
    w_down,
):
    tp_count = lax.axis_size("tp")
    rep_count = lax.axis_size("rep")
    width = w_query.shape[2]
    inner = w_gate.shape[2]
    head_size = D // HEADS
    shards = (w_query, w_key, w_value, w_out, w_gate, w_up, w_down)
    share_rows = tokens.shape[0]
    fits = (
        rep_count == 2 * PLANE
        and share_rows == VIEWS * HW
        and time_ids.shape[0] == tp_count
        and inner == PLANE * width
        and w_query.shape[1] % 8 == 0
    )
    if fits:
        here = lax.axis_index("tp")
        cond = set_conditioning(
            lax.dynamic_slice_in_dim(view_ids, here, 1, 0),
            lax.dynamic_slice_in_dim(time_ids, here, 1, 0),
            camera_table,
        )
        return fused_blocks(tokens, cond, norm_attn, norm_ffn, shards, tp_count)

    row_ids = lax.axis_index("tp") * share_rows + jnp.arange(share_rows, dtype=jnp.int32)
    stream = tokens.astype(jnp.float32) + conditioning(row_ids, view_ids, time_ids, camera_table)

    def whole_weight(layer_index, first, count, after):
        own = [shard[layer_index] for shard in shards[first : first + count]]
        own, _ = lax.optimization_barrier((own, after))
        return lax.all_gather(jnp.concatenate(own, axis=1), ("rep", "tp"), axis=0, tiled=True)

    for layer_index in range(LAYERS):
        normed = layer_norm(stream, norm_attn[layer_index])
        qkv_w = whole_weight(layer_index, 0, 3, normed)
        packed = jnp.dot(normed, qkv_w, preferred_element_type=jnp.float32).astype(jnp.bfloat16)
        mixed_rows = attend(packed, head_size)
        stream = stream + out_terms(mixed_rows, whole_weight(layer_index, 3, 1, mixed_rows))
        normed = layer_norm(stream, norm_ffn[layer_index])
        gate_w = whole_weight(layer_index, 4, 1, normed)
        gate_part = jnp.dot(normed, gate_w, preferred_element_type=jnp.float32)
        up_w = whole_weight(layer_index, 5, 1, gate_part)
        up_part = jnp.dot(normed, up_w, preferred_element_type=jnp.float32)
        hidden = (jax.nn.gelu(gate_part, approximate=False) * up_part).astype(jnp.bfloat16)
        stream = stream + out_terms(hidden, whole_weight(layer_index, 6, 1, hidden))
    return stream.astype(jnp.bfloat16)


def solution(mesh):
    return jax.shard_map(
        body,
        mesh=mesh,
        in_specs=(
            P(("rep", "tp"), None),
            P("rep", None),
            P("rep"),
            P(),
            P(),
            P(),
            P(None, ("rep", "tp"), None),
            P(None, ("rep", "tp"), None),
            P(None, ("rep", "tp"), None),
            P(None, ("rep", "tp"), None),
            P(None, ("rep", "tp"), None),
            P(None, ("rep", "tp"), None),
            P(None, ("rep", "tp"), None),
        ),
        out_specs=P(("rep", "tp"), None),
        check_vma=False,
    )
```

time: 470 us -> 382 us (0.81)
  Pallas kernels: 427 us -> 376 us
  matrix products: 31.7 us -> 1.75 us
  other arithmetic: 5.37 us -> 0.13 us
    pallas_call x3 -> x1, Pallas kernels: 427 us -> 376 us  [fused_blocks(): pl.pallas_call(functools.partial(fused_kernel, shape), out_shape=jax.Shap...]
    dot_general x7 -> x1, matrix products: 27.3 us -> 1.75 us  [set_conditioning(): camera = jnp.dot(onehot_pose, camera_table, precision=lax.Precision.HIGHEST)]
where the time goes in v1:
time: 382 us; the launch traced here: 381 us
  Pallas kernels  376 us (98%)
    pallas_call x1, Pallas kernels, fused_blocks(): pl.pallas_call(functools.partial(fused_kernel, shape), out_shape=jax.Shap...  376 us

profile of v1, /device:TPU:0, one launch (start us, length us, event | category | flops | bytes accessed | tf_op | source)
XLA Modules:
  0.0 381.5 jit_solution(15945869627241827006)
XLA Ops:
  0.0 0.0 copy-start
  0.0 0.0 copy-start.1
  0.0 0.7 copy-done.1
  0.7 0.6 dynamic_slice.7
  1.9 0.0 copy-done
  1.9 0.1 fusion
  2.1 1.7 convolution_add_fusion.cond_ref
  3.8 375.7 %fused_blocks.1 = bf16[256,1280]{1,0:T(8,128)(2,1)} custom-call(bf16[256,1280]{1,0:T(8,128)(2,1)} %tokens_ref.1, f32[4,1280]{1,0:T(4,128)} %convolution_add_fusion.cond_ref, f32[2,1280]{1,0:T(2,128)} %gain_attn_ref.1, f32[2,1280]{1,0:T(2,128)} %gain_ffn_ref.1, bf16[2,40,1280]{2,1,0:T(8,128)(2,1)} %wq_ref.1, bf16[2,40,1280]{2,1,0:T(8,128)(2,1)} %wk_ref.1, ...), custom_call_target="tpu_custom_call" | custom-call | tf_op jit(solution)/shard_map/fused_blocks/pallas_call | solution.py:633
  379.5 2.0 copy.15
  (2 shorter events, 0.0 us)
Async XLA Ops:
  0.0 1.9 copy-start
  0.0 0.7 copy-start.1

commit v2 on v1

--- a/solution.py
+++ b/solution.py
@@ -49,7 +49,34 @@
 
 MESH = pl.DeviceIdType.MESH
 LANES = 128
+ATTN, FFN = range(2)
+(
+    LINE,
+    OUT,
+    NEAR,
+    FAR,
+    COLUMNS,
+    PAIRS_ATTN,
+    PAIRS_FFN,
+    EMBED,
+    NORM,
+    PROJECT,
+    MIX,
+    PROJECT_OUT,
+    ROWS_OUT,
+    ROWS_ON,
+    ROWS_IN,
+    ROWS_DONE,
+    TILES,
+    TERM,
+    TERM_IN,
+    RESIDUAL,
+) = range(20)
 PLANE = 4
+POOL = 96
+NAMED = 12
+PARTS = ((0, 3), (3, 4))
+SLOTS = (0, 2, 1, 3)
 
 
 class Pieces:
@@ -57,6 +84,7 @@
         self.chips_z, self.layers, self.tile_count = chips_z, layers, tile_count
         self.send_sems = send_sems
         self.used = 0
+        self.named = 0
         self.finish = []
         rep_here = lax.axis_index("rep")
         self.z = lax.axis_index("tp")
@@ -81,17 +109,24 @@
         return self.at(self.q, self.core, self.z + step)
 
     def copy(self, source, target, arrived, device, condition=None, later=True):
+        if later:
+            if len(self.finish) == POOL:
+                guarded(*self.finish.pop(0))
+            place = self.used % POOL
+            self.used += 1
+        else:
+            place = POOL + self.named % NAMED
+            self.named += 1
         one = pltpu.make_async_remote_copy(
             src_ref=source,
             dst_ref=target,
-            send_sem=self.send_sems.at[self.used],
+            send_sem=self.send_sems.at[place],
             recv_sem=arrived,
             device_id=device,
             device_id_type=MESH,
         )
-        self.used += 1
         if later:
-            self.finish.append((condition, one))
+            self.finish.append((condition, one.wait_send))
         return one
 
     def arrival(self, region, arrived):
@@ -121,7 +156,9 @@
 def fused_kernel(
     shape,
     tokens_ref,
-    cond_ref,
+    view_ids_ref,
+    time_ids_ref,
+    table_ref,
     gain_attn_ref,
     gain_ffn_ref,
     wq_ref,
@@ -154,8 +191,11 @@
     rows = stream.shape[0]
     here = core * chips_z + z
 
-    def attn_piece(layer, q_from, core_from, z_from):
-        return full.at[layer, 0:4, q_from, core_from * chips_z + z_from]
+    def attn_piece(layer, part, q_from, core_from, z_from):
+        first_kind, last_kind = PARTS[part]
+        return full.at[
+            layer, first_kind:last_kind, q_from, core_from * chips_z + z_from
+        ]
 
     def ffn_piece(layer, part, core_from, z_from):
         return full.at[
@@ -172,10 +212,12 @@
 
     own = []
     for layer in range(layers):
-        group = []
-        for kind, ref in enumerate((wq_ref, wk_ref, wv_ref, wo_ref)):
-            group.append((ref.at[layer], full.at[layer, kind, q, here]))
-        own.append(group)
+        for first_kind, last_kind in PARTS:
+            group = []
+            for kind in range(first_kind, last_kind):
+                ref = (wq_ref, wk_ref, wv_ref, wo_ref)[kind]
+                group.append((ref.at[layer], full.at[layer, kind, q, here]))
+            own.append(group)
     for layer in range(layers):
         group = []
         for kind, ref in enumerate((wg_ref, wu_ref, wd_ref)):
@@ -237,20 +279,22 @@
 
         guarded(valid, action)
 
-    def attn_line(layer, offset):
+    def attn_line(layer, part, offset):
+        stage = layer * len(PARTS) + part
         along_line(
-            layer,
-            attn_piece(layer, q, core, z + offset),
-            pair_attn_sems.at[layer, q, z + offset],
+            stage,
+            attn_piece(layer, part, q, core, z + offset),
+            pair_attn_sems.at[stage],
             offset,
         )
 
-    def attn_plane(layer, offset):
+    def attn_plane(layer, part, offset):
+        stage = layer * len(PARTS) + part
         z_from = z + offset
         valid = in_line(offset)
-        region = attn_piece(layer, q, core, z_from)
+        region = attn_piece(layer, part, q, core, z_from)
         sends = [
-            net.copy(region, region, plane_sems.at[layer, q, z_from], net.peer(peer), valid)
+            net.copy(region, region, plane_sems.at[stage, q, z_from], net.peer(peer), valid)
             for peer in (net.first, net.second)
         ]
 
@@ -260,19 +304,18 @@
 
         guarded(valid, action)
 
-    def from_plane(layer, offset, which):
+    def from_plane(layer, part, offset, which):
+        stage = layer * len(PARTS) + part
         z_from = z + offset
         valid = in_line(offset)
         peer = (net.first, net.second, net.diagonal)[which]
-        region = attn_piece(layer, peer, core, z_from)
-        arrived = plane_sems.at[layer, peer, z_from]
+        region = attn_piece(layer, part, peer, core, z_from)
+        arrived = plane_sems.at[stage, peer, z_from]
         sends = []
         if which == 0:
             sends.append(net.copy(region, region, arrived, net.peer(net.second), valid))
         sends.append(
-            net.copy(
-                region, region, pair_attn_sems.at[layer, peer, z_from], net.sibling(), valid
-            )
+            net.copy(region, region, pair_attn_sems.at[stage], net.sibling(), valid)
         )
 
         def action():
@@ -282,16 +325,12 @@
 
         guarded(valid, action)
 
-    def attn_pairs(layer):
-        def wait_one(index, carry):
-            q_from, z_from = index // chips_z, index % chips_z
-            net.arrival(
-                attn_piece(layer, q_from, 1 - core, z_from),
-                pair_attn_sems.at[layer, q_from, z_from],
-            )
-            return carry
-
-        lax.fori_loop(0, PLANE * chips_z, wait_one, 0)
+    def attn_pairs(layer, part):
+        first_kind, last_kind = PARTS[part]
+        net.arrival(
+            full.at[layer, first_kind:last_kind, :, pl.ds((1 - core) * chips_z, chips_z)],
+            pair_attn_sems.at[layer * len(PARTS) + part],
+        )
 
     def exchange_columns(layer):
         for peer in (net.first, net.second, net.diagonal):
@@ -304,104 +343,50 @@
                 ).start()
 
     def columns_here(layer):
-        wait_local(layers + layer)
+        wait_local(layers * len(PARTS) + layer)
         for peer in (net.first, net.second, net.diagonal):
             net.arrival(full.at[layer, 4:7, peer, here], share_sems.at[layer, peer])
 
     def ffn_line(layer, part, offset):
         along_line(
-            layers + layer * tile_count + part,
+            layers * len(PARTS) + layer * tile_count + part,
             ffn_piece(layer, part, core, z + offset),
-            pair_ffn_sems.at[layer * tile_count + part, z + offset],
+            pair_ffn_sems.at[layer * tile_count + part],
             offset,
         )
 
     def ffn_pairs(layer, part):
-        for z_from in range(chips_z):
-            net.arrival(
-                ffn_piece(layer, part, 1 - core, z_from),
-                pair_ffn_sems.at[layer * tile_count + part, z_from],
-            )
+        span = pl.ds(part * tile, tile)
+        net.arrival(
+            full.at[layer, 4:7, :, pl.ds((1 - core) * chips_z, chips_z), :, span],
+            pair_ffn_sems.at[layer * tile_count + part],
+        )
 
     def offsets(hops):
         return [hops, -hops] if hops else [0]
 
-    steps = []
-    for layer in range(layers):
-        steps.append(("attn", layer, 0))
-    for layer in range(layers):
-        for part in range(tile_count):
-            steps.append(("ffn", layer, part))
-
-    def send_own(step):
-        kind, layer, part = step
-        if kind == "attn":
-            wait_local(layer)
-            attn_line(layer, 0)
-        else:
-            if part == 0:
-                columns_here(layer)
-            ffn_line(layer, part, 0)
-
-    def pass_on(step, hops):
-        kind, layer, part = step
-        for offset in offsets(hops):
-            if kind == "attn":
-                attn_line(layer, offset)
-            else:
-                ffn_line(layer, part, offset)
-
-    queue = []
-    for index, step in enumerate(steps):
-        if index == 0:
-            queue.append((step, 0))
-        for hops in range(1, chips_z):
-            if hops == 2 and index + 1 < len(steps):
-                queue.append((steps[index + 1], 0))
-            queue.append((step, hops))
-    done = [0]
-
-    def pump(amount):
-        for _ in range(amount):
-            if done[0] < len(queue):
-                step, hops = queue[done[0]]
-                done[0] += 1
-                if hops == 0:
-                    send_own(step)
-                else:
-                    pass_on(step, hops)
-
-    def pump_until(step):
-        while (step, chips_z - 1) in queue[done[0] :]:
-            pump(1)
-
-    plane_queue = []
-    for layer in range(layers):
-        items = []
-        for hops in range(chips_z):
-            items.append((2 * hops, "out", layer, hops))
-            items.append((2 * hops + 1, "near", layer, hops))
-            items.append((2 * hops + 2.5, "far", layer, hops))
-        items.sort(key=lambda item: item[0])
-        plane_queue.append(items)
-    plane_done = [0] * layers
-
-    def spread(layer, amount):
-        for _ in range(amount):
-            if plane_done[layer] == len(plane_queue[layer]):
-                return
-            _, what, _, hops = plane_queue[layer][plane_done[layer]]
-            plane_done[layer] += 1
-            for offset in offsets(hops):
-                if what == "out":
-                    attn_plane(layer, offset)
-                elif what == "near":
-                    from_plane(layer, offset, 0)
-                    from_plane(layer, offset, 1)
-                else:
-                    from_plane(layer, offset, 2)
+    def offsets(hops):
+        return [hops, -hops] if hops else [0]
 
     chunk = 64 if rows % 64 == 0 else rows
+
+    def embed():
+        views = view_ids_ref.shape[1]
+        per_view = rows // views
+        half_width = width // 2
+        place = lax.broadcasted_iota(jnp.int32, (1, half_width), 1).astype(jnp.float32)
+        frequency = jnp.exp(-math.log(10000.0) * place / half_width)
+        angles = time_ids_ref[z].astype(jnp.float32) * frequency
+        code = jnp.concatenate([jnp.cos(angles), jnp.sin(angles)], axis=1)
+        pose = lax.broadcasted_iota(jnp.int32, (table_ref.shape[0], 1), 0)
+        for view in range(views):
+            span = pl.ds(view * per_view, per_view)
+            camera = jnp.sum(
+                jnp.where(pose == view_ids_ref[z, view], table_ref[...], 0.0),
+                axis=0,
+                keepdims=True,
+            )
+            stream[span, :] = tokens_ref[span, :].astype(jnp.float32) + (camera + code)
 
     def normalise(gain_ref, layer):
         def one(index, carry):
@@ -459,142 +444,85 @@
 
         lax.fori_loop(0, width // column, one, 0)
 
-    def ffn_tile(layer, part, place):
-        gate = jnp.dot(
-            normed[place], weight(layer, 4, part, tile), preferred_element_type=jnp.float32
-        )
-        up = jnp.dot(
-            normed[place], weight(layer, 5, part, tile), preferred_element_type=jnp.float32
-        )
+    half = rows // 2
+
+    def ffn_tile(layer, part, unit):
+        pair = pl.ds(unit % 2 * 2, 2)
+        span = pl.ds(pl.multiple_of(unit // 2 * half, half), half)
+        acts = normed[pair, span, :].reshape(2 * half, width)
+        gate = jnp.dot(acts, weight(layer, 4, part, tile), preferred_element_type=jnp.float32)
+        up = jnp.dot(acts, weight(layer, 5, part, tile), preferred_element_type=jnp.float32)
         gate = 0.5 * gate * (1.0 + lax.erf(gate * math.sqrt(0.5)))
         hidden = (gate * up).astype(jnp.bfloat16)
-        term = out_terms(hidden, weight(layer, 6, part, tile))
+        term = out_terms(hidden, weight(layer, 6, part, tile)).reshape(2, half, width)
         if part == 0:
-            total[place] = term
+            total[pair, span, :] = term
         else:
-            total[place] = total[place] + term
-
-    pump(1)
-    spread(0, 1)
-    exchange_columns(0)
-    views = cond_ref.shape[0]
-    per_view = rows // views
-    for view in range(views):
-        span = pl.ds(view * per_view, per_view)
-        stream[span, :] = tokens_ref[span, :].astype(jnp.float32) + cond_ref[view : view + 1, :]
-    normalise(gain_attn_ref, 0)
-
-    pump(1)
-    spread(0, 1)
-    pump(2)
-    spread(0, 2)
-    spread(0, 1)
-    pump(1)
-    spread(0, 2)
-    pump(1)
-    spread(0, 2)
-    pump(1)
-    spread(0, 20)
-    pump(1)
-    attn_pairs(0)
-
-    for layer in range(layers):
-        last_layer = layer == layers - 1
-        if layer:
-            pump_until(("attn", layer, 0))
-            spread(layer, 20)
-            attn_pairs(layer)
-            normalise(gain_attn_ref, layer)
-        project(layer, 0)
-        project(layer, 1)
-        project(layer, 2)
-        pump(1)
-        if not last_layer:
-            pump_until(("attn", layer + 1, 0))
-            exchange_columns(layer + 1)
-            spread(layer + 1, 3)
-        attend_heads(0, D // head_size)
-        pump(1)
-        project_out(layer)
-        normalise(gain_ffn_ref, layer)
-
-        rows_sent = [
+            total[pair, span, :] = total[pair, span, :] + term
+
+    def head_of(part):
+        count = D // head_size
+        return count * part // 2
+
+    rows_sent, terms_sent = [], []
+
+    def half_span(index):
+        return pl.ds(index * half, half)
+
+    def send_rows(layer, index, role, target, side):
+        span = half_span(index)
+        rows_sent.append(
             net.copy(
-                normed.at[0],
-                normed.at[1 + side],
-                rows_sems.at[layer, side],
+                normed.at[SLOTS[role], span],
+                normed.at[SLOTS[target], span],
+                rows_sems.at[layer, index, target - 1],
                 net.peer((net.first, net.second)[side]),
                 later=False,
             )
-            for side in range(2)
-        ]
-        for one in rows_sent:
-            one.start()
-        pump(2)
-        net.arrival(normed.at[1], rows_sems.at[layer, 0])
-        rows_sent.append(
+        )
+        rows_sent[-1].start()
+
+    def rows_arrival(layer, index, role):
+        net.arrival(
+            normed.at[SLOTS[role], half_span(index)], rows_sems.at[layer, index, role - 1]
+        )
+
+    def term_arrival(layer, index, target):
+        net.arrival(
+            landing.at[target, half_span(index)], term_sems.at[layer, index, target]
+        )
+
+    def send_term(layer, index, target):
+        span = half_span(index)
+        role = (3, 1, 2)[target]
+        value = total[SLOTS[role], span, :]
+        if target == 2:
+            term_arrival(layer, index, 0)
+            value = value + landing[0, span, :].astype(jnp.float32)
+        staging[target, span, :] = value.astype(jnp.bfloat16)
+        terms_sent.append(
             net.copy(
-                normed.at[1],
-                normed.at[3],
-                rows_sems.at[layer, 2],
-                net.peer(net.second),
+                staging.at[target, span],
+                landing.at[target, span],
+                term_sems.at[layer, index, target],
+                net.peer((net.first, net.first, net.second)[target]),
                 later=False,
             )
         )
-        rows_sent[-1].start()
-        if not last_layer:
-            spread(layer + 1, 3)
-        pump(1)
-        net.arrival(normed.at[2], rows_sems.at[layer, 1])
-        pump(1)
-
-        for part in range(tile_count - 1):
-            pump_until(("ffn", layer, part))
-            ffn_pairs(layer, part)
-            if part == 0:
-                net.arrival(normed.at[3], rows_sems.at[layer, 2])
-
-            def one(place, carry, part=part):
-                ffn_tile(layer, part, place)
-                return carry
-
-            lax.fori_loop(0, PLANE, one, 0)
-        for sent in rows_sent:
-            sent.wait_send()
-        part = tile_count - 1
-        pump_until(("ffn", layer, part))
-        ffn_pairs(layer, part)
-
-        terms_sent = []
-
-        def send_term(slot, target, arrived, peer):
-            terms_sent.append(
-                net.copy(
-                    staging.at[slot], landing.at[target], arrived, net.peer(peer), later=False
-                )
-            )
-            terms_sent[-1].start()
-
-        ffn_tile(layer, part, 3)
-        staging[0] = total[3].astype(jnp.bfloat16)
-        send_term(0, 0, term_sems.at[layer, 0], net.first)
-        ffn_tile(layer, part, 1)
-        staging[1] = total[1].astype(jnp.bfloat16)
-        send_term(1, 1, term_sems.at[layer, 1], net.first)
-        ffn_tile(layer, part, 2)
-        net.arrival(landing.at[0], term_sems.at[layer, 0])
-        staging[2] = (total[2] + landing[0].astype(jnp.float32)).astype(jnp.bfloat16)
-        send_term(2, 2, term_sems.at[layer, 2], net.second)
-        ffn_tile(layer, part, 0)
-        pump(2)
-        net.arrival(landing.at[1], term_sems.at[layer, 1])
-        pump(1)
-        net.arrival(landing.at[2], term_sems.at[layer, 2])
-
-        def add(index, carry, last_layer=last_layer):
+        terms_sent[-1].start()
+
+    def settle(copies):
+        for one in copies:
+            one.wait_send()
+        copies.clear()
+
+    def residual(layer):
+        last_layer = layer == layers - 1
+
+        def add(index, carry):
             span = pl.ds(pl.multiple_of(index * chunk, chunk), chunk)
             summed = stream[span, :] + (
-                total[0, span, :]
+                total[SLOTS[0], span, :]
                 + landing[1, span, :].astype(jnp.float32)
                 + landing[2, span, :].astype(jnp.float32)
             )
@@ -605,11 +533,188 @@
             return carry
 
         lax.fori_loop(0, rows // chunk, add, 0)
-        for sent in terms_sent:
-            sent.wait_send()
-
-    for condition, one in net.finish:
-        guarded(condition, one.wait_send)
+        settle(terms_sent)
+
+    def piece(kind, layer, part, hops):
+        if kind == ATTN:
+            if hops == 0:
+                wait_local(layer * len(PARTS) + part)
+            for offset in offsets(hops):
+                attn_line(layer, part, offset)
+        else:
+            if hops == 0 and part == 0:
+                columns_here(layer)
+            for offset in offsets(hops):
+                ffn_line(layer, part, offset)
+
+    def tiles(layer, part, first_unit, last_unit):
+        if last_unit - first_unit == 1:
+            ffn_tile(layer, part, first_unit)
+            return
+
+        def one(unit, carry):
+            ffn_tile(layer, part, unit)
+            return carry
+
+        lax.fori_loop(first_unit, last_unit, one, 0)
+
+    def run(token):
+        name, rest = token[0], token[1:]
+        if name == LINE:
+            piece(*rest)
+        elif name == OUT:
+            for offset in offsets(rest[2]):
+                attn_plane(rest[0], rest[1], offset)
+        elif name == NEAR:
+            for offset in offsets(rest[2]):
+                from_plane(rest[0], rest[1], offset, 0)
+                from_plane(rest[0], rest[1], offset, 1)
+        elif name == FAR:
+            for offset in offsets(rest[2]):
+                from_plane(rest[0], rest[1], offset, 2)
+        elif name == COLUMNS:
+            exchange_columns(rest[0])
+        elif name == PAIRS_ATTN:
+            attn_pairs(*rest)
+        elif name == PAIRS_FFN:
+            ffn_pairs(*rest)
+        elif name == EMBED:
+            embed()
+        elif name == NORM:
+            normalise((gain_attn_ref, gain_ffn_ref)[rest[1]], rest[0])
+        elif name == PROJECT:
+            project(*rest)
+        elif name == MIX:
+            attend_heads(head_of(rest[1]), head_of(rest[1] + 1))
+        elif name == PROJECT_OUT:
+            project_out(rest[0])
+        elif name == ROWS_OUT:
+            send_rows(rest[0], rest[1], 0, 1, 0)
+            send_rows(rest[0], rest[1], 0, 2, 1)
+        elif name == ROWS_ON:
+            rows_arrival(rest[0], rest[1], 1)
+            send_rows(rest[0], rest[1], 1, 3, 1)
+        elif name == ROWS_IN:
+            rows_arrival(*rest)
+        elif name == ROWS_DONE:
+            settle(rows_sent)
+        elif name == TILES:
+            tiles(*rest)
+        elif name == TERM:
+            send_term(*rest)
+        elif name == TERM_IN:
+            term_arrival(*rest)
+        elif name == RESIDUAL:
+            residual(rest[0])
+
+    for token in schedule(chips_z, layers, tile_count):
+        run(token)
+    for condition, action in net.finish:
+        guarded(condition, action)
+
+
+def merged(tokens):
+    out = []
+    for token in tokens:
+        if token[0] == TILES:
+            layer, part, index, first_pair, count = token[1:]
+            first = 2 * index + first_pair
+            token = (TILES, layer, part, first, first + count)
+            previous = out[-1]
+            if previous[:3] == token[:3] and previous[4] == first:
+                out[-1] = previous[:4] + (first + count,)
+                continue
+        out.append(token)
+    return out
+
+
+def schedule(chips_z, layers, tile_count):
+    if (chips_z, layers, tile_count) == (4, 2, 5):
+        return merged(ORDER)
+    return merged(plain_schedule(chips_z, layers, tile_count))
+
+
+def plain_schedule(chips_z, layers, tile_count):
+    tokens = [(COLUMNS, 0), (EMBED,), (NORM, 0, 0)]
+    for layer in range(layers):
+        if layer:
+            tokens.append((COLUMNS, layer))
+        for part in range(len(PARTS)):
+            for hops in range(chips_z):
+                tokens += [(LINE, ATTN, layer, part, hops), (OUT, layer, part, hops)]
+                tokens += [(NEAR, layer, part, hops), (FAR, layer, part, hops)]
+            tokens.append((PAIRS_ATTN, layer, part))
+        if layer:
+            tokens.append((NORM, layer, 0))
+        tokens += [(PROJECT, layer, kind) for kind in range(3)]
+        tokens += [(MIX, layer, 0), (MIX, layer, 1), (PROJECT_OUT, layer)]
+        tokens.append((NORM, layer, 1))
+        tokens += [(ROWS_OUT, layer, 0), (ROWS_OUT, layer, 1)]
+        for index in range(2):
+            tokens += [(ROWS_ON, layer, index), (ROWS_IN, layer, index, 2)]
+            tokens.append((ROWS_IN, layer, index, 3))
+        for part in range(tile_count):
+            tokens += [(LINE, FFN, layer, part, hops) for hops in range(chips_z)]
+            tokens.append((PAIRS_FFN, layer, part))
+            tokens += [(TILES, layer, part, index, 0, 2) for index in range(2)]
+        tokens.append((ROWS_DONE, layer))
+        for target in range(3):
+            tokens += [(TERM, layer, index, target) for index in range(2)]
+        for target in (1, 2):
+            tokens += [(TERM_IN, layer, index, target) for index in range(2)]
+        tokens.append((RESIDUAL, layer))
+    return tokens
+
+
+ORDER = (
+    (LINE, ATTN, 0, 0, 0), (LINE, ATTN, 1, 0, 0), (LINE, ATTN, 0, 1, 0), (OUT, 0, 1, 0),
+    (COLUMNS, 0), (LINE, ATTN, 0, 0, 1), (OUT, 0, 0, 0), (LINE, ATTN, 1, 1, 0),
+    (LINE, ATTN, 0, 1, 1), (OUT, 0, 0, 1), (LINE, ATTN, 1, 0, 1), (LINE, ATTN, 0, 0, 2),
+    (OUT, 0, 0, 2), (OUT, 0, 1, 1), (LINE, ATTN, 0, 1, 2), (EMBED,), (NEAR, 0, 0, 1),
+    (OUT, 0, 1, 2), (LINE, ATTN, 1, 1, 1), (LINE, FFN, 0, 0, 0), (OUT, 1, 0, 0),
+    (LINE, ATTN, 0, 0, 3), (LINE, FFN, 0, 1, 0), (LINE, ATTN, 0, 1, 3), (OUT, 0, 0, 3),
+    (LINE, ATTN, 1, 0, 2), (NEAR, 0, 1, 2), (LINE, FFN, 0, 0, 1), (NEAR, 0, 0, 3),
+    (OUT, 0, 1, 3), (NEAR, 0, 0, 0), (NEAR, 0, 0, 2), (LINE, FFN, 0, 1, 1), (LINE, FFN, 0, 0, 2),
+    (NEAR, 0, 1, 0), (FAR, 0, 0, 0), (NEAR, 0, 1, 1), (NEAR, 0, 1, 3), (NEAR, 1, 0, 0),
+    (NORM, 0, 0), (FAR, 0, 0, 1), (COLUMNS, 1), (OUT, 1, 1, 0), (LINE, FFN, 0, 4, 0),
+    (OUT, 1, 0, 1), (FAR, 0, 1, 0), (LINE, ATTN, 1, 1, 2), (FAR, 0, 1, 2), (LINE, FFN, 0, 2, 0),
+    (FAR, 0, 0, 3), (FAR, 0, 0, 2), (PAIRS_ATTN, 0, 0), (LINE, ATTN, 1, 0, 3), (PROJECT, 0, 0),
+    (PROJECT, 0, 1), (FAR, 0, 1, 3), (PROJECT, 0, 2), (FAR, 0, 1, 1), (MIX, 0, 0), (MIX, 0, 1),
+    (PAIRS_ATTN, 0, 1), (LINE, FFN, 0, 4, 1), (OUT, 1, 0, 3), (LINE, FFN, 0, 3, 0),
+    (PROJECT_OUT, 0), (NORM, 0, 1), (LINE, FFN, 0, 2, 1), (LINE, FFN, 0, 0, 3),
+    (LINE, FFN, 0, 4, 2), (ROWS_OUT, 0, 0), (PAIRS_FFN, 0, 0), (LINE, FFN, 0, 3, 1),
+    (LINE, ATTN, 1, 1, 3), (ROWS_OUT, 0, 1), (LINE, FFN, 0, 2, 2), (ROWS_ON, 0, 1),
+    (LINE, FFN, 0, 1, 2), (ROWS_ON, 0, 0), (ROWS_IN, 0, 1, 3), (LINE, FFN, 0, 2, 3),
+    (NEAR, 1, 0, 3), (LINE, FFN, 0, 1, 3), (ROWS_IN, 0, 1, 2), (OUT, 1, 0, 2),
+    (LINE, FFN, 0, 3, 2), (LINE, FFN, 1, 0, 0), (TILES, 0, 0, 1, 0, 2), (PAIRS_FFN, 0, 2),
+    (ROWS_IN, 0, 0, 3), (LINE, FFN, 0, 4, 3), (NEAR, 1, 0, 1), (LINE, FFN, 1, 1, 0),
+    (ROWS_IN, 0, 0, 2), (PAIRS_FFN, 0, 1), (FAR, 1, 0, 0), (LINE, FFN, 1, 2, 0),
+    (LINE, FFN, 1, 3, 0), (FAR, 1, 0, 3), (TILES, 0, 0, 0, 0, 2), (ROWS_DONE, 0),
+    (LINE, FFN, 1, 4, 0), (OUT, 1, 1, 2), (TILES, 0, 1, 0, 0, 2), (PAIRS_FFN, 0, 4),
+    (TILES, 0, 1, 1, 0, 2), (LINE, FFN, 0, 3, 3), (NEAR, 1, 0, 2), (TILES, 0, 2, 1, 0, 2),
+    (PAIRS_FFN, 0, 3), (OUT, 1, 1, 3), (TILES, 0, 3, 1, 0, 2), (TILES, 0, 4, 1, 1, 1),
+    (FAR, 1, 0, 1), (TERM, 0, 1, 1), (TERM, 0, 1, 0), (TILES, 0, 2, 0, 0, 2),
+    (TILES, 0, 3, 0, 0, 2), (TILES, 0, 4, 0, 1, 1), (TILES, 0, 4, 1, 0, 1), (TERM, 0, 0, 0),
+    (NEAR, 1, 1, 0), (NEAR, 1, 1, 3), (LINE, FFN, 1, 2, 1), (TILES, 0, 4, 0, 0, 1),
+    (FAR, 1, 0, 2), (TERM, 0, 1, 2), (LINE, FFN, 1, 0, 1), (TERM, 0, 0, 2), (TERM, 0, 0, 1),
+    (TERM_IN, 0, 1, 1), (LINE, FFN, 1, 1, 1), (OUT, 1, 1, 1), (TERM_IN, 0, 0, 2),
+    (TERM_IN, 0, 0, 1), (TERM_IN, 0, 1, 2), (FAR, 1, 1, 3), (LINE, FFN, 1, 4, 1),
+    (PAIRS_ATTN, 1, 0), (LINE, FFN, 1, 3, 1), (RESIDUAL, 0), (NORM, 1, 0), (NEAR, 1, 1, 2),
+    (PROJECT, 1, 0), (NEAR, 1, 1, 1), (LINE, FFN, 1, 0, 2), (PROJECT, 1, 1), (FAR, 1, 1, 0),
+    (FAR, 1, 1, 2), (LINE, FFN, 1, 2, 2), (PROJECT, 1, 2), (FAR, 1, 1, 1), (MIX, 1, 0),
+    (MIX, 1, 1), (PAIRS_ATTN, 1, 1), (PROJECT_OUT, 1), (NORM, 1, 1), (ROWS_OUT, 1, 0),
+    (LINE, FFN, 1, 1, 2), (LINE, FFN, 1, 3, 2), (LINE, FFN, 1, 2, 3), (ROWS_ON, 1, 0),
+    (ROWS_OUT, 1, 1), (LINE, FFN, 1, 0, 3), (PAIRS_FFN, 1, 0), (ROWS_IN, 1, 0, 3),
+    (LINE, FFN, 1, 1, 3), (LINE, FFN, 1, 4, 2), (PAIRS_FFN, 1, 2), (ROWS_IN, 1, 0, 2),
+    (TILES, 1, 0, 0, 0, 2), (ROWS_ON, 1, 1), (LINE, FFN, 1, 3, 3), (PAIRS_FFN, 1, 1),
+    (TILES, 1, 1, 0, 0, 2), (TILES, 1, 2, 0, 0, 2), (ROWS_IN, 1, 1, 2), (LINE, FFN, 1, 4, 3),
+    (PAIRS_FFN, 1, 3), (TILES, 1, 3, 0, 0, 2), (PAIRS_FFN, 1, 4), (TILES, 1, 4, 0, 1, 1),
+    (ROWS_IN, 1, 1, 3), (ROWS_DONE, 1), (TERM, 1, 0, 0), (TILES, 1, 0, 1, 0, 2),
+    (TILES, 1, 4, 0, 0, 1), (TERM, 1, 0, 1), (TILES, 1, 1, 1, 0, 2), (TILES, 1, 2, 1, 0, 2),
+    (TERM, 1, 0, 2), (TILES, 1, 3, 1, 0, 2), (TILES, 1, 4, 1, 1, 1), (TERM, 1, 1, 0),
+    (TILES, 1, 4, 1, 0, 1), (TERM, 1, 1, 1), (TERM, 1, 1, 2), (TERM_IN, 1, 1, 2),
+    (TERM_IN, 1, 0, 1), (TERM_IN, 1, 1, 1), (TERM_IN, 1, 0, 2), (RESIDUAL, 1),
+)
 
 
 def head_window(head_size):
@@ -617,23 +722,23 @@
     return -(-reach // LANES) * LANES
 
 
-def fused_blocks(tokens, cond, norm_attn, norm_ffn, shards, chips_z):
+def fused_blocks(tokens, view_ids, time_ids, camera_table, norm_attn, norm_ffn, shards, chips_z):
     layers, share, width = shards[0].shape
     inner = shards[4].shape[2]
     tile = 256 if width % 256 == 0 else LANES
     tile_count = width // tile
     rows = tokens.shape[0]
     head_size = D // HEADS
-    stages = layers * (1 + tile_count)
-    sends = 1024
+    stages = layers * (len(PARTS) + tile_count)
     shape = (layers, chips_z, width, tile, tile_count, head_size)
     anywhere = pl.BlockSpec(memory_space=pl.ANY)
     inside = pl.BlockSpec(memory_space=pltpu.VMEM)
+    scalars = pl.BlockSpec(memory_space=pltpu.SMEM)
     kind = tokens.dtype
     return pl.pallas_call(
         functools.partial(fused_kernel, shape),
         out_shape=jax.ShapeDtypeStruct((rows, width), kind),
-        in_specs=[inside] * 4 + [anywhere] * 7,
+        in_specs=[inside, scalars, scalars] + [inside] * 3 + [anywhere] * 7,
         out_specs=inside,
         scratch_shapes=[
             pltpu.VMEM((layers, 7, PLANE, 2 * chips_z, share, width), kind),
@@ -643,20 +748,20 @@
             pltpu.VMEM((PLANE, rows, width), jnp.float32),
             pltpu.VMEM((rows, width), jnp.float32),
             pltpu.SemaphoreType.DMA((layers * 7,)),
-            pltpu.SemaphoreType.DMA((sends,)),
+            pltpu.SemaphoreType.DMA((POOL + NAMED,)),
             pltpu.SemaphoreType.DMA((stages, chips_z)),
-            pltpu.SemaphoreType.DMA((layers, PLANE, chips_z)),
+            pltpu.SemaphoreType.DMA((layers * len(PARTS), PLANE, chips_z)),
             pltpu.SemaphoreType.DMA((layers, PLANE)),
-            pltpu.SemaphoreType.DMA((layers, PLANE, chips_z)),
-            pltpu.SemaphoreType.DMA((layers * tile_count, chips_z)),
-            pltpu.SemaphoreType.DMA((layers, 3)),
-            pltpu.SemaphoreType.DMA((layers, 3)),
+            pltpu.SemaphoreType.DMA((layers * len(PARTS),)),
+            pltpu.SemaphoreType.DMA((layers * tile_count,)),
+            pltpu.SemaphoreType.DMA((layers, 2, 3)),
+            pltpu.SemaphoreType.DMA((layers, 2, 3)),
         ],
         compiler_params=pltpu.CompilerParams(
             collective_id=0, has_side_effects=True, vmem_limit_bytes=67_000_000
         ),
         name="fused_blocks",
-    )(tokens, cond, norm_attn, norm_ffn, *shards)
+    )(tokens, view_ids, time_ids, camera_table, norm_attn, norm_ffn, *shards)
 
 
 def attend(packed, head_size):
@@ -688,13 +793,6 @@
     return lax.dot_general(
         mixed_rows, weight, (((1,), (1,)), ((), ())), preferred_element_type=jnp.float32
     )
-
-
-def set_conditioning(view_ids, time_ids, camera_table):
-    pose_range = jnp.arange(camera_table.shape[0], dtype=jnp.int32)
-    onehot_pose = (view_ids[0][:, None] == pose_range[None, :]).astype(jnp.float32)
-    camera = jnp.dot(onehot_pose, camera_table, precision=lax.Precision.HIGHEST)
-    return camera + time_code(time_ids, camera_table.shape[1])
 
 
 def body(
@@ -725,15 +823,12 @@
         and time_ids.shape[0] == tp_count
         and inner == PLANE * width
         and w_query.shape[1] % 8 == 0
+        and share_rows % 32 == 0
     )
     if fits:
-        here = lax.axis_index("tp")
-        cond = set_conditioning(
-            lax.dynamic_slice_in_dim(view_ids, here, 1, 0),
-            lax.dynamic_slice_in_dim(time_ids, here, 1, 0),
-            camera_table,
-        )
-        return fused_blocks(tokens, cond, norm_attn, norm_ffn, shards, tp_count)
+        return fused_blocks(
+            tokens, view_ids, time_ids, camera_table, norm_attn, norm_ffn, shards, tp_count
+        )
 
     row_ids = lax.axis_index("tp") * share_rows + jnp.arange(share_rows, dtype=jnp.int32)
     stream = tokens.astype(jnp.float32) + conditioning(row_ids, view_ids, time_ids, camera_table)

time: 382 us -> 249 us (0.65)
  Pallas kernels: 376 us -> 247 us
    pallas_call x1, Pallas kernels: 376 us -> 247 us  [fused_blocks(): pl.pallas_call(functools.partial(fused_kernel, shape), out_shape=jax.Shap...]
where the time goes in v2:
time: 249 us
  Pallas kernels  247 us (99%)
    pallas_call x1, Pallas kernels, fused_blocks(): pl.pallas_call(functools.partial(fused_kernel, shape), out_shape=jax.Shap...  247 us

profile of v2, /device:TPU:0, one launch (start us, length us, event | category | flops | bytes accessed | tf_op | source)
XLA Modules:
  0.0 249.0 jit_solution(12388227432738235395)
XLA Ops:
  0.0 247.0 %fused_blocks.1 = bf16[256,1280]{1,0:T(8,128)(2,1)} custom-call(bf16[256,1280]{1,0:T(8,128)(2,1)} %tokens_ref.1, s32[4,4]{1,0:T(4,128)} %view_ids_ref.1, s32[4]{0:T(128)} %time_ids_ref.1, f32[32,1280]{1,0:T(8,128)} %table_ref.1, f32[2,1280]{1,0:T(2,128)} %gain_attn_ref.1, f32[2,1280]{1,0:T(2,128)} %gain_ffn_ref.1, bf16[2,40,1280]{2,1,0:T(8,128)(2,1)} %wq_ref.1, ...), custom_call_target="tpu_custom_call" | custom-call | tf_op jit(solution)/shard_map/fused_blocks/pallas_call | solution.py:738
  247.0 2.0 copy.15

commit v3 on v2

--- a/solution.py
+++ b/solution.py
@@ -73,7 +73,7 @@
     RESIDUAL,
 ) = range(20)
 PLANE = 4
-POOL = 96
+POOL = 48
 NAMED = 12
 PARTS = ((0, 3), (3, 4))
 SLOTS = (0, 2, 1, 3)
@@ -175,7 +175,10 @@
     staging,
     total,
     stream,
+    tokens_in,
+    table_in,
     own_sems,
+    first_sems,
     send_sems,
     line_sems,
     plane_sems,
@@ -234,6 +237,13 @@
             slot += 1
         local.append(copies)
 
+    fetches = (
+        pltpu.make_async_copy(tokens_ref, tokens_in, first_sems.at[0]),
+        pltpu.make_async_copy(table_ref, table_in, first_sems.at[1]),
+    )
+    for one in fetches:
+        one.start()
+
     def wait_local(index):
         for one in local[index]:
             one.wait()
@@ -379,14 +389,18 @@
         angles = time_ids_ref[z].astype(jnp.float32) * frequency
         code = jnp.concatenate([jnp.cos(angles), jnp.sin(angles)], axis=1)
         pose = lax.broadcasted_iota(jnp.int32, (table_ref.shape[0], 1), 0)
+        for one in fetches:
+            one.wait()
+        groups = per_view // tokens_in.shape[1]
         for view in range(views):
             span = pl.ds(view * per_view, per_view)
             camera = jnp.sum(
-                jnp.where(pose == view_ids_ref[z, view], table_ref[...], 0.0),
+                jnp.where(pose == view_ids_ref[z, view], table_in[...], 0.0),
                 axis=0,
                 keepdims=True,
             )
-            stream[span, :] = tokens_ref[span, :].astype(jnp.float32) + (camera + code)
+            part = tokens_in[view * groups : (view + 1) * groups].reshape(per_view, width)
+            stream[span, :] = part.astype(jnp.float32) + (camera + code)
 
     def normalise(gain_ref, layer):
         def one(index, carry):
@@ -738,7 +752,7 @@
     return pl.pallas_call(
         functools.partial(fused_kernel, shape),
         out_shape=jax.ShapeDtypeStruct((rows, width), kind),
-        in_specs=[inside, scalars, scalars] + [inside] * 3 + [anywhere] * 7,
+        in_specs=[anywhere, scalars, scalars, anywhere] + [inside] * 2 + [anywhere] * 7,
         out_specs=inside,
         scratch_shapes=[
             pltpu.VMEM((layers, 7, PLANE, 2 * chips_z, share, width), kind),
@@ -747,7 +761,10 @@
             pltpu.VMEM((3, rows, width), kind),
             pltpu.VMEM((PLANE, rows, width), jnp.float32),
             pltpu.VMEM((rows, width), jnp.float32),
+            pltpu.VMEM((rows // 8, 8, width), kind),
+            pltpu.VMEM(camera_table.shape, camera_table.dtype),
             pltpu.SemaphoreType.DMA((layers * 7,)),
+            pltpu.SemaphoreType.DMA((2,)),
             pltpu.SemaphoreType.DMA((POOL + NAMED,)),
             pltpu.SemaphoreType.DMA((stages, chips_z)),
             pltpu.SemaphoreType.DMA((layers * len(PARTS), PLANE, chips_z)),
@@ -761,7 +778,15 @@
             collective_id=0, has_side_effects=True, vmem_limit_bytes=67_000_000
         ),
         name="fused_blocks",
-    )(tokens, view_ids, time_ids, camera_table, norm_attn, norm_ffn, *shards)
+    )(
+        tokens.reshape(rows // 8, 8, width),
+        view_ids,
+        time_ids,
+        camera_table,
+        norm_attn,
+        norm_ffn,
+        *shards,
+    )
 
 
 def attend(packed, head_size):

time: 249 us -> 248 us (level)
  no operation moved by 1% of the time
where the time goes in v3:
time: 248 us
  Pallas kernels  246 us (99%)
    pallas_call x1, Pallas kernels, fused_blocks(): pl.pallas_call(functools.partial(fused_kernel, shape), out_shape=jax.Shap...  246 us

profile of v3, /device:TPU:0, one launch (start us, length us, event | category | flops | bytes accessed | tf_op | source)
XLA Modules:
  0.0 247.9 jit_solution(12808077978930024058)
XLA Ops:
  0.0 245.9 %fused_blocks.1 = bf16[256,1280]{1,0:T(8,128)(2,1)} custom-call(bf16[32,8,1280]{2,1,0:T(8,128)(2,1)} %bitcast.1, s32[4,4]{1,0:T(4,128)} %view_ids_ref.1, s32[4]{0:T(128)} %time_ids_ref.1, f32[32,1280]{1,0:T(8,128)} %table_ref.1, f32[2,1280]{1,0:T(2,128)} %gain_attn_ref.1, f32[2,1280]{1,0:T(2,128)} %gain_ffn_ref.1, bf16[2,40,1280]{2,1,0:T(8,128)(2,1)} %wq_ref.1, ...), custom_call_target="tpu_custom_call" | custom-call | tf_op jit(solution)/shard_map/fused_blocks/pallas_call | solution.py:752
  245.9 2.0 copy.15
